TPU v7x, 128 devices: a whole 4x4x4 slice. The times are simulated.
128 devices in a mesh: rows: 64 (over z, y, x), grp: 2 (over core).
Axes of the slice: x: 4, y: 4, z: 4, core: 2. Of those that a mesh axis runs over, the one named last changes fastest.
Arguments:
- earlier: bfloat16 [524288, 1024], P(('rows', 'grp')), may hold values from -6 to 6
- snapshots: bfloat16 [524288, 512], P(('rows', 'grp')), may hold values from -8 to 8
- later: bfloat16 [524288, 512], P(('rows', 'grp')), may hold values from -8 to 8
Outputs:
- basis: bfloat16 [524288, 512], P(('rows', 'grp'))
- factors: float32 [2, 256, 256], replicated
- shift_block: float32 [512, 512], replicated
All inputs are finite; a program needn't handle non-finite values.
Results may differ from a plain program's by a relative error of at most 0.0045.
The roundings to bfloat16 on the way count: a program that leaves them out, or rounds other values in their place, can miss the bound.
Values sent between devices are 32-bit elements; how exact they have to be, the bound alone decides.
A program may use at most 128 MiB of HBM per device.

v0:
```python
import jax
import jax.numpy as jnp
from jax import lax
from jax.sharding import Mesh
from jax.sharding import PartitionSpec as P

PANEL = 256
ROWS = ("rows_0", "rows_1", "rows_2")
ROWS_GRP = ("rows_0", "rows_1", "rows_2", "grp")


def in_blocks(value, dim, length):
    lengths = value.shape
    tiles = value.reshape(*lengths[:dim], length, lengths[dim] // length, *lengths[dim + 1 :])
    return jnp.moveaxis(tiles, dim, 0)


def sent_and_summed(value, axis, dim):
    tiles = in_blocks(value, dim, lax.axis_size(axis))
    arrived = lax.all_to_all(tiles, axis, split_axis=0, concat_axis=0, tiled=True)
    return arrived.sum(axis=0)


def summed_rows(value, axes, dim):
    far, near = axes
    tiles = in_blocks(value, dim, lax.axis_size(far))
    nearer = sent_and_summed(tiles, near, dim + 1)
    arrived = lax.all_to_all(nearer, far, split_axis=0, concat_axis=0, tiled=True)
    return arrived.sum(axis=0)


def filled_up(lines, length):
    spare = -len(lines) % length
    return jnp.pad(lines, [(0, spare)] + [(0, 0)] * (lines.ndim - 1))


def copy_for_each(value, axis):
    copies = jnp.broadcast_to(value, (lax.axis_size(axis), *value.shape))
    return lax.all_to_all(copies, axis, split_axis=0, concat_axis=0, tiled=True)


def in_order(tiles, dim):
    tiles = jnp.moveaxis(tiles, 0, dim)
    lengths = tiles.shape
    return tiles.reshape(*lengths[:dim], lengths[dim] * lengths[dim + 1], *lengths[dim + 2 :])


def whole_of(value, axes, dim):
    far, near = axes
    tiles = copy_for_each(copy_for_each(value, far), near)
    return in_order(tiles.swapaxes(0, 1).reshape(-1, *value.shape), dim)


def sum_by_parts(value, axes):
    lines = value.reshape(-1, value.shape[-1])
    own = summed_rows(filled_up(lines, lax.axis_size(axes[0]) * lax.axis_size(axes[1])), axes, 0)
    whole = whole_of(own, axes, 0)
    return whole[: len(lines)].reshape(value.shape)


def inner(left, right):
    return jnp.einsum("rk,rc->kc", left, right, preferred_element_type=jnp.float32)


def applied(space, coeffs):
    return jnp.dot(space, coeffs.astype(jnp.bfloat16), preferred_element_type=jnp.float32)


def factor(gram, second):
    lower = jnp.linalg.cholesky(gram)
    inverse = jax.scipy.linalg.solve_triangular(
        lower, jnp.eye(gram.shape[0], dtype=jnp.float32), lower=True
    )
    newcols = jnp.dot(second, inverse.T, precision=lax.Precision.HIGHEST).astype(jnp.bfloat16)
    return (newcols, lower.T, inverse)


def body(earlier, snapshots, later):
    total = earlier.shape[0] * lax.axis_size(ROWS) * lax.axis_size("grp")
    panel_one = snapshots[:, :PANEL]
    panel_two = snapshots[:, PANEL:]
    both = sum_by_parts(inner(earlier, snapshots), (("rows_0", "rows_1", "rows_2"), "grp")) / total
    first = both[:, :PANEL]
    early_two = both[:, PANEL:]
    once = (panel_one.astype(jnp.float32) - applied(earlier, first)).astype(jnp.bfloat16)
    second = sum_by_parts(inner(earlier, once), (("rows_0", "rows_1", "rows_2"), "grp")) / total
    twice = once.astype(jnp.float32) - applied(earlier, second)
    local_gram = jnp.dot(twice.T, twice, precision=lax.Precision.HIGHEST)
    gram = sum_by_parts(local_gram, (("rows_0", "rows_1", "rows_2"), "grp")) / total
    q_first, r_first, unused_inverse = factor(gram, twice)
    space = jnp.concatenate([earlier, q_first], axis=1)
    fresh = sum_by_parts(inner(q_first, panel_two), (("rows_0", "rows_1", "rows_2"), "grp")) / total
    first = jnp.concatenate([early_two, fresh], axis=0)
    once = (panel_two.astype(jnp.float32) - applied(space, first)).astype(jnp.bfloat16)
    second = sum_by_parts(inner(space, once), (("rows_0", "rows_1", "rows_2"), "grp")) / total
    twice = once.astype(jnp.float32) - applied(space, second)
    local_gram = jnp.dot(twice.T, twice, precision=lax.Precision.HIGHEST)
    gram = sum_by_parts(local_gram, (("rows_0", "rows_1", "rows_2"), "grp")) / total
    q_second, r_second, inverse = factor(gram, twice)
    basis = jnp.concatenate([q_first, q_second], axis=1)
    shift_block = sum_by_parts(inner(basis, later), (("rows_0", "rows_1", "rows_2"), "grp")) / total
    return (basis, jnp.stack([r_first, r_second]), shift_block)


def solution(mesh):
    torus = Mesh(
        mesh.devices.reshape(4, 4, 4, mesh.shape["grp"]), ("rows_0", "rows_1", "rows_2", "grp")
    )
    return jax.shard_map(
        body,
        mesh=torus,
        in_specs=(P(ROWS_GRP, None), P(ROWS_GRP, None), P(ROWS_GRP, None)),
        out_specs=(P(ROWS_GRP, None), P(), P()),
        check_vma=False,
    )
```

profile of v0, /device:TPU:1, one launch (start us, length us, event | category | flops | bytes accessed | tf_op | source)
XLA Modules:
  0.0 558.4 jit_solution(16205451131761304538)
XLA Ops:
  0.6 8.2 %fusion.51 = f32[1024,512]{1,0:T(8,128)S(1)} fusion(bf16[4096,1024]{1,0:T(8,128)(2,1)} %param.6, bf16[4096,512]{1,0:T(8,128)(2,1)} %param.7), kind=kOutput, calls=%fused_computation.107 | convolution fusion | flops 4294967296 | bytes 14680064 | tf_op jit(solution)/shard_map/rk,rc->kc/dot_general | solution.py:62
  18.3 29.2 %all_to_all.153 = f32[64,8,512]{2,1,0:T(8,128)} all-to-all(f32[64,8,512]{2,1,0:T(8,128)S(1)} %reduce_sum.126), channel_id=1, replica_groups=mesh['rows_0'=4,'rows_1'=4,'rows_2'=4,'grp'=2] {'rows_0','rows_1','rows_2'}, dimensions={0} | all-to-all | bytes 2097152 | tf_op jit(solution)/shard_map/all_to_all | solution.py:28
  57.6 13.9 %all-to-all-done.2 = f32[64,8,512]{2,1,0:T(8,128)S(1)} async-done(((f32[64,8,512]{2,1,0:T(8,128)}), f32[64,8,512]{2,1,0:T(8,128)S(1)}, u32[]{:S(2)}, u32[]{:S(2)}) %all-to-all-start.2) | async-done | bytes 1048608 | tf_op jit(solution)/shard_map/all_to_all | solution.py:39
  71.8 8.2 %all_to_all.140 = f32[2,64,8,512]{3,2,1,0:T(8,128)S(1)} all-to-all(f32[2,64,8,512]{3,2,1,0:T(8,128)S(1)} %broadcast_in_dim.44), channel_id=1, replica_groups=mesh['rows_0'=4,'rows_1'=4,'rows_2'=4,'grp'=2] {'grp'}, dimensions={0} | all-to-all | bytes 4194304 | tf_op jit(solution)/shard_map/all_to_all | solution.py:39
  95.2 16.5 %all_to_all.154 = f32[64,8,256]{2,1,0:T(8,128)S(1)} all-to-all(f32[64,8,256]{2,1,0:T(8,128)S(1)} %reduce_sum.128), channel_id=1, replica_groups=mesh['rows_0'=4,'rows_1'=4,'rows_2'=4,'grp'=2] {'rows_0','rows_1','rows_2'}, dimensions={0} | all-to-all | bytes 1048576 | tf_op jit(solution)/shard_map/all_to_all | solution.py:28
  111.8 15.7 %all_to_all.155 = f32[64,8,256]{2,1,0:T(8,128)S(1)} all-to-all(f32[64,8,256]{2,1,0:T(8,128)S(1)} %broadcast_in_dim.45), channel_id=1, replica_groups=mesh['rows_0'=4,'rows_1'=4,'rows_2'=4,'grp'=2] {'rows_0','rows_1','rows_2'}, dimensions={0} | all-to-all | bytes 1048576 | tf_op jit(solution)/shard_map/all_to_all | solution.py:39
  150.7 13.0 %all_to_all.156 = f32[64,2,256]{2,1,0:T(2,128)S(1)} all-to-all(f32[64,2,256]{2,1,0:T(2,128)S(1)} %reduce_sum.130), channel_id=1, replica_groups=mesh['rows_0'=4,'rows_1'=4,'rows_2'=4,'grp'=2] {'rows_0','rows_1','rows_2'}, dimensions={0} | all-to-all | bytes 262144 | tf_op jit(solution)/shard_map/all_to_all | solution.py:28
  169.5 8.7 %all-to-all-done.10 = f32[64,2,256]{2,1,0:T(2,128)S(1)} async-done(((f32[64,2,256]{2,1,0:T(2,128)}), f32[64,2,256]{2,1,0:T(2,128)S(1)}, u32[]{:S(2)}, u32[]{:S(2)}) %all-to-all-start.10) | async-done | bytes 131104 | tf_op jit(solution)/shard_map/all_to_all | solution.py:39
  185.6 11.7 %cholesky.130 = f32[128,128]{1,0:T(8,128)S(1)} custom-call(f32[128,128]{1,0:T(8,128)S(1)} %cholesky.194), custom_call_target="Cholesky" | custom-call | tf_op jit(solution)/shard_map/jit(cholesky)/cholesky | solution.py:70
  197.3 9.8 %custom-call.13 = f32[1,128,128]{1,2,0:T(8,128)S(1)} custom-call(f32[1,128,128]{2,1,0:T(8,128)S(1)} %get-tuple-element.76), custom_call_target="InvertDiagBlocksLowerTriangular" | custom-call | tf_op jit(solution)/shard_map/jit(cholesky)/cholesky | solution.py:70
  207.6 11.7 %cholesky.147 = f32[128,128]{1,0:T(8,128)S(1)} custom-call(f32[128,128]{1,0:T(8,128)S(1)} %convolution_subtract_fusion.5), custom_call_target="Cholesky" | custom-call | tf_op jit(solution)/shard_map/jit(cholesky)/cholesky | solution.py:70
  226.2 19.9 %custom-call.14 = f32[2,128,128]{1,2,0:T(8,128)S(1)} custom-call(f32[2,128,128]{2,1,0:T(8,128)S(1)} %get-tuple-element.19), custom_call_target="InvertDiagBlocksLowerTriangular" | custom-call | tf_op jit(solution)/shard_map/jit(_solve_triangular)/triangular_solve | solution.py:71
  261.3 13.2 %all_to_all.157 = f32[64,2,256]{2,1,0:T(2,128)S(1)} all-to-all(f32[64,2,256]{2,1,0:T(2,128)S(1)} %reduce_sum.132), channel_id=1, replica_groups=mesh['rows_0'=4,'rows_1'=4,'rows_2'=4,'grp'=2] {'rows_0','rows_1','rows_2'}, dimensions={0} | all-to-all | bytes 262144 | tf_op jit(solution)/shard_map/all_to_all | solution.py:28
  322.0 22.5 %all_to_all.158 = f32[64,10,256]{2,1,0:T(8,128)S(1)} all-to-all(f32[64,10,256]{2,1,0:T(8,128)S(1)} %copy.144), channel_id=1, replica_groups=mesh['rows_0'=4,'rows_1'=4,'rows_2'=4,'grp'=2] {'rows_0','rows_1','rows_2'}, dimensions={0} | all-to-all | bytes 1310720 | tf_op jit(solution)/shard_map/all_to_all | solution.py:28
  344.7 21.0 %all_to_all.159 = f32[64,10,256]{2,1,0:T(8,128)S(1)} all-to-all(f32[64,10,256]{2,1,0:T(8,128)S(1)} %broadcast_in_dim.51), channel_id=1, replica_groups=mesh['rows_0'=4,'rows_1'=4,'rows_2'=4,'grp'=2] {'rows_0','rows_1','rows_2'}, dimensions={0} | all-to-all | bytes 1310720 | tf_op jit(solution)/shard_map/all_to_all | solution.py:39
  366.2 7.7 %all_to_all.148 = f32[2,64,10,256]{3,1,2,0:T(8,128)S(1)} all-to-all(f32[2,64,10,256]{3,1,2,0:T(8,128)S(1)} %broadcast_in_dim.52), channel_id=1, replica_groups=mesh['rows_0'=4,'rows_1'=4,'rows_2'=4,'grp'=2] {'grp'}, dimensions={0} | all-to-all | bytes 2621440 | tf_op jit(solution)/shard_map/all_to_all | solution.py:39
  395.2 12.9 %all_to_all.160 = f32[64,2,256]{2,1,0:T(2,128)S(1)} all-to-all(f32[64,2,256]{2,1,0:T(2,128)S(1)} %reduce_sum.136), channel_id=1, replica_groups=mesh['rows_0'=4,'rows_1'=4,'rows_2'=4,'grp'=2] {'rows_0','rows_1','rows_2'}, dimensions={0} | all-to-all | bytes 262144 | tf_op jit(solution)/shard_map/all_to_all | solution.py:28
  408.2 13.5 %all_to_all.161 = f32[64,2,256]{2,1,0:T(2,128)S(1)} all-to-all(f32[64,2,256]{2,1,0:T(2,128)S(1)} %broadcast_in_dim.53), channel_id=1, replica_groups=mesh['rows_0'=4,'rows_1'=4,'rows_2'=4,'grp'=2] {'rows_0','rows_1','rows_2'}, dimensions={0} | all-to-all | bytes 262144 | tf_op jit(solution)/shard_map/all_to_all | solution.py:39
  429.1 11.7 %cholesky.164 = f32[128,128]{1,0:T(8,128)S(1)} custom-call(f32[128,128]{1,0:T(8,128)S(1)} %cholesky.197), custom_call_target="Cholesky" | custom-call | tf_op jit(solution)/shard_map/jit(cholesky)/cholesky | solution.py:70
  440.9 9.8 %custom-call.15 = f32[1,128,128]{1,2,0:T(8,128)S(1)} custom-call(f32[1,128,128]{2,1,0:T(8,128)S(1)} %get-tuple-element.72), custom_call_target="InvertDiagBlocksLowerTriangular" | custom-call | tf_op jit(solution)/shard_map/jit(cholesky)/cholesky | solution.py:70
  451.2 11.7 %cholesky.181 = f32[128,128]{1,0:T(8,128)S(1)} custom-call(f32[128,128]{1,0:T(8,128)S(1)} %convolution_subtract_fusion.4), custom_call_target="Cholesky" | custom-call | tf_op jit(solution)/shard_map/jit(cholesky)/cholesky | solution.py:70
  470.4 19.9 %custom-call.16 = f32[2,128,128]{1,2,0:T(8,128)S(1)} custom-call(f32[2,128,128]{2,1,0:T(8,128)S(1)} %get-tuple-element.20), custom_call_target="InvertDiagBlocksLowerTriangular" | custom-call | tf_op jit(solution)/shard_map/jit(_solve_triangular)/triangular_solve | solution.py:71
  491.2 11.5 %convolution_convert_fusion = bf16[4096,256]{0,1:T(8,128)(2,1)S(1)} fusion(f32[4096,256]{1,0:T(8,128)} %copy-done.1, f32[128,256]{1,0:T(8,128)S(1)} %fusion.34, f32[128,256]{1,0:T(8,128)S(1)} %fusion.29), kind=kOutput, calls=%fused_computation.9 | convolution fusion | flops 3222339584 | bytes 6553600 | tf_op jit(solution)/shard_map/dot_general | solution.py:74
  521.5 10.4 %all-to-all-done.25 = f32[64,4,512]{2,1,0:T(4,128)S(1)} async-done(((f32[64,4,512]{2,1,0:T(4,128)}), f32[64,4,512]{2,1,0:T(4,128)S(1)}, u32[]{:S(2)}, u32[]{:S(2)}) %all-to-all-start.25) | async-done | bytes 524320 | tf_op jit(solution)/shard_map/all_to_all | solution.py:28
  (179 shorter events, 229.4 us)
Async XLA Ops:
  10.4 7.6 %all-to-all-start = ((f32[2,64,8,512]{3,2,1,0:T(8,128)}), f32[2,64,8,512]{3,2,1,0:T(8,128)S(1)}, u32[]{:S(2)}, u32[]{:S(2)}) async-start(f32[2,64,8,512]{3,2,1,0:T(8,128)} %bitcast.135), calls=%async_computation | async-start | bytes 4194304 | tf_op jit(solution)/shard_map/all_to_all | solution.py:20
  47.5 7.2 %slice-start = ((bf16[4096,512]{1,0:T(8,128)(2,1)}), bf16[4096,256]{1,0:T(8,128)(2,1)S(1)}, s32[]{:S(2)}) async-start(bf16[4096,512]{1,0:T(8,128)(2,1)} %param.7), calls=%async_computation.28 | async-start | bytes 4194304 | tf_op jit(solution)/shard_map/slice | solution.py:80
  50.1 21.5 %all-to-all-start.2 = ((f32[64,8,512]{2,1,0:T(8,128)}), f32[64,8,512]{2,1,0:T(8,128)S(1)}, u32[]{:S(2)}, u32[]{:S(2)}) async-start(f32[64,8,512]{2,1,0:T(8,128)} %broadcast_in_dim.43), calls=%async_computation.2 | async-start | bytes 2097152 | tf_op jit(solution)/shard_map/all_to_all | solution.py:39
  71.8 8.6 %copy-start.7 = (bf16[4096,256]{0,1:T(8,128)(2,1)S(1)}, bf16[4096,256]{0,1:T(8,128)(2,1)}, u32[]{:S(2)}) copy-start(bf16[4096,256]{0,1:T(8,128)(2,1)} %copy.160) | copy-start | bytes 6291460
  80.0 7.7 %slice-start.1 = ((s8[8388608]{0:T(1024)(128)(4,1)}), s8[4194304]{0:T(1024)(128)(4,1)S(1)}, s32[]{:S(2)}) async-start(s8[8388608]{0:T(1024)(128)(4,1)} %bitcast.146), calls=%async_computation.29 | async-start | bytes 8388608
  80.3 7.3 %slice-start.2 = ((s8[8388608]{0:T(1024)(128)(4,1)}), s8[4194304]{0:T(1024)(128)(4,1)S(1)}, s32[]{:S(2)}) async-start(s8[8388608]{0:T(1024)(128)(4,1)} %bitcast.146), calls=%async_computation.30 | async-start | bytes 8388608
  86.4 1.3 copy-start.11
  111.8 23.2 %copy-start.12 = (bf16[4096,256]{0,1:T(8,128)(2,1)S(1)}, bf16[4096,256]{0,1:T(8,128)(2,1)}, u32[]{:S(2)}) copy-start(bf16[4096,256]{0,1:T(8,128)(2,1)} %copy-done.11) | copy-start | bytes 6291460
  140.8 2.0 copy-start
  164.5 13.7 %all-to-all-start.10 = ((f32[64,2,256]{2,1,0:T(2,128)}), f32[64,2,256]{2,1,0:T(2,128)S(1)}, u32[]{:S(2)}, u32[]{:S(2)}) async-start(f32[64,2,256]{2,1,0:T(2,128)} %broadcast_in_dim.47), calls=%async_computation.10 | async-start | bytes 262144 | tf_op jit(solution)/shard_map/all_to_all | solution.py:39
  169.5 77.2 %copy-start.4 = (f32[256,256]{1,0:T(8,128)}, f32[256,256]{1,0:T(8,128)S(1)}, u32[]{:S(2)}) copy-start(f32[256,256]{1,0:T(8,128)S(1)} %fusion.25) | copy-start | bytes 786436
  246.1 8.4 %copy-start.3 = (bf16[4096,512]{1,0:T(8,128)(2,1)S(1)}, bf16[4096,512]{1,0:T(8,128)(2,1)}, u32[]{:S(2)}) copy-start(bf16[4096,512]{1,0:T(8,128)(2,1)} %param.7) | copy-start | bytes 12582916
  275.3 13.7 %all-to-all-start.14 = ((f32[64,2,256]{2,1,0:T(2,128)}), f32[64,2,256]{2,1,0:T(2,128)S(1)}, u32[]{:S(2)}, u32[]{:S(2)}) async-start(f32[64,2,256]{2,1,0:T(2,128)} %broadcast_in_dim.49), calls=%async_computation.14 | async-start | bytes 262144 | tf_op jit(solution)/shard_map/all_to_all | solution.py:39
  281.1 15.2 %copy-start.9 = (bf16[1024,256]{1,0:T(8,128)(2,1)S(1)}, bf16[1024,256]{1,0:T(8,128)(2,1)}, u32[]{:S(2)}) copy-start(bf16[1024,256]{1,0:T(8,128)(2,1)} %slice.65) | copy-start | bytes 1572868
  296.3 8.3 %copy-start.6 = (bf16[4096,256]{1,0:T(8,128)(2,1)S(1)}, bf16[4096,256]{1,0:T(8,128)(2,1)}, u32[]{:S(2)}) copy-start(bf16[4096,256]{1,0:T(8,128)(2,1)} %copy.139) | copy-start | bytes 6291460
  303.2 1.4 copy-start.13
  381.9 2.0 copy-start.1
  390.9 99.4 %copy-start.5 = (f32[256,256]{1,0:T(8,128)S(1)}, f32[256,256]{1,0:T(8,128)}, u32[]{:S(2)}) copy-start(f32[256,256]{1,0:T(8,128)} %copy-done.4) | copy-start | bytes 786436
  490.3 13.8 %copy-start.10 = (bf16[4096,512]{1,0:T(8,128)(2,1)S(1)}, bf16[4096,512]{1,0:T(8,128)(2,1)}, u32[]{:S(2)}) copy-start(bf16[4096,512]{1,0:T(8,128)(2,1)} %param.8) | copy-start | bytes 12582916
  502.8 1.3 copy-start.2
  507.4 12.1 %copy-start.8 = (f32[1,256,256]{1,2,0:T(8,128)S(1)}, f32[1,256,256]{1,2,0:T(8,128)}, u32[]{:S(2)}) copy-start(f32[1,256,256]{1,2,0:T(8,128)} %get-tuple-element.65) | copy-start | bytes 786436
  514.8 17.1 %all-to-all-start.25 = ((f32[64,4,512]{2,1,0:T(4,128)}), f32[64,4,512]{2,1,0:T(4,128)S(1)}, u32[]{:S(2)}, u32[]{:S(2)}) async-start(f32[64,4,512]{2,1,0:T(4,128)} %reduce_sum.138), calls=%async_computation.25 | async-start | bytes 1048576 | tf_op jit(solution)/shard_map/all_to_all | solution.py:28
  532.9 15.9 %all-to-all-start.26 = ((f32[64,4,512]{2,1,0:T(4,128)}), f32[64,4,512]{2,1,0:T(4,128)S(1)}, u32[]{:S(2)}, u32[]{:S(2)}) async-start(f32[64,4,512]{2,1,0:T(4,128)} %broadcast_in_dim.55), calls=%async_computation.26 | async-start | bytes 1048576 | tf_op jit(solution)/shard_map/all_to_all | solution.py:39
where the time goes:
time: 568 us; the launch traced here: 558 us
  blocking collectives  234 us (41%)
  other arithmetic  121 us (21%)
  matrix products  78.7 us (14%)
  local copies, waits for them, and re-layouts  48.8 us (9%)
  waiting for transfers between devices  42 us (7%)
  starting transfers between devices  28.9 us (5%)
    all_to_all x6, blocking collectives, summed_rows(): lax.all_to_all(nearer, far, split_axis=0, concat_axis=0, tiled=True)  108 us
    all_to_all x10, blocking collectives, copy_for_each(): return lax.all_to_all(copies, axis, split_axis=0, concat_axis=0, tiled=True)  101 us
    another operation x13, other arithmetic, factor(): lower = jnp.linalg.cholesky(gram)  68.5 us
    another operation x3, other arithmetic, factor(): jax.scipy.linalg.solve_triangular(lower, jnp.eye(gram.shape[0], dtype=jnp...  39.8 us
    all_to_all x4, waiting for transfers between devices, copy_for_each(): return lax.all_to_all(copies, axis, split_axis=0, concat_axis=0, tiled=True)  29 us
    all_to_all x6, blocking collectives, sent_and_summed(): lax.all_to_all(tiles, axis, split_axis=0, concat_axis=0, tiled=True)  25.9 us
    dot_general x4, matrix products, applied(): jnp.dot(space, coeffs.astype(jnp.bfloat16), preferred_element_type=jnp.fl...  25 us
    dot_general x5, matrix products, inner(): jnp.einsum('rk,rc->kc', left, right, preferred_element_type=jnp.float32)  21.7 us
  transfers between devices with their start and end apart: 6, of which 6 were waited for; matrix products, arithmetic and copies ran while one was open for 3% of the time, Pallas kernels for 0%

commit v1 on v0

v1 whole, which is shorter than its diff:
```python
import functools
import itertools

import jax
import jax.numpy as jnp
from jax import lax
from jax.experimental import pallas as pl
from jax.experimental.pallas import tpu as pltpu
from jax.sharding import Mesh
from jax.sharding import PartitionSpec as P

PANEL = 256
BLOCK = 32
HALF = 128
AXES = ("rows_0", "rows_1", "rows_2", "grp")


def thirds(value):
    top = value.astype(jnp.bfloat16)
    rest = value - top.astype(jnp.float32)
    middle = rest.astype(jnp.bfloat16)
    low = (rest - middle.astype(jnp.float32)).astype(jnp.bfloat16)
    return top, middle, low


def halves(value):
    top = value.astype(jnp.bfloat16)
    return top, (value - top.astype(jnp.float32)).astype(jnp.bfloat16)


MESH = pl.DeviceIdType.MESH


def offsets(stage):
    sizes = [2 if axis == "grp" else 4 for axis in stage]
    return [o for o in itertools.product(*[range(s) for s in sizes]) if any(o)]


def peer_of(stage, offset):
    return {
        axis: lax.rem(lax.axis_index(axis) + shift, 2 if axis == "grp" else 4)
        for axis, shift in zip(stage, offset)
        if shift
    }


def place_in(stage, offset=None):
    place = 0
    for n, axis in enumerate(stage):
        size = 2 if axis == "grp" else 4
        at = lax.axis_index(axis)
        if offset is not None:
            at = lax.rem(at + offset[n], size)
        place = place * size + at
    return place


def size_of(stage):
    size = 1
    for axis in stage:
        size *= 2 if axis == "grp" else 4
    return size


def sum_kernel(colors, x_ref, o_ref, *scratch):
    it = iter(scratch)
    state = []
    for start, rows, stages in colors:
        levels = []
        length = rows
        for stage in stages:
            length //= size_of(stage)
            levels.append((stage, offsets(stage), length, next(it), next(it), next(it), next(it), next(it), next(it)))
        state.append((start, levels))
    greeted = []
    for _, levels in state:
        for level in levels:
            for offset in level[1]:
                key = tuple(sorted((a, o) for a, o in zip(level[0], offset) if o))
                if key not in greeted:
                    greeted.append(key)
    barrier = pltpu.get_barrier_semaphore()
    for key in greeted:
        pl.semaphore_signal(barrier, inc=1, device_id=peer_of([a for a, _ in key], [o for _, o in key]), device_id_type=MESH)
    pl.semaphore_wait(barrier, len(greeted))

    depth = max(len(levels) for _, levels in state)
    pending = []
    where = [start for start, _ in state]
    live = [None] * len(state)

    def finish(c, s):
        stage, offs, length, slots, acc = state[c][1][s][:5]
        own = pl.multiple_of(place_in(stage) * length, 8)
        for copy in live[c]:
            copy.wait_recv()
        src = x_ref if s == 0 else state[c][1][s - 1][4]
        base = where[c] if s == 0 else 0
        value = src[pl.ds(pl.multiple_of(base + own, 8), length), :]
        for n in range(len(offs)):
            value = value + slots[n]
        where[c] = where[c] + own
        last = s + 1 == len(state[c][1])
        if last:
            o_ref[pl.ds(pl.multiple_of(where[c], 8), length), :] = value
        else:
            acc[...] = value

    for s in range(depth + 1):
        for c, (start, levels) in enumerate(state):
            if s > 0 and s <= len(levels):
                finish(c, s - 1)
            if s < len(levels):
                stage, offs, length, slots, acc, send, recv, _, _ = levels[s]
                src = x_ref if s == 0 else levels[s - 1][4]
                base = start if s == 0 else 0
                live[c] = []
                for n, offset in enumerate(offs):
                    at = pl.multiple_of(base + place_in(stage, offset) * length, 8)
                    copy = pltpu.make_async_remote_copy(
                        src_ref=src.at[pl.ds(at, length), :], dst_ref=slots.at[n],
                        send_sem=send.at[n], recv_sem=recv.at[n],
                        device_id=peer_of(stage, offset), device_id_type=MESH)
                    copy.start()
                    live[c].append(copy)
                    pending.append(copy)
    gath = [None] * len(state)
    for s in range(depth + 1):
        for c, (start, levels) in enumerate(state):
            k = len(levels) - 1 - s
            if s > 0 and s <= len(levels):
                for copy in gath[c]:
                    copy.wait_recv()
                stage, _, length = levels[k + 1][:3]
                where[c] = where[c] - place_in(stage) * length
            if k >= 0:
                stage, offs, length, _, _, _, _, send, recv = levels[k]
                gath[c] = []
                at = pl.multiple_of(where[c], 8)
                for n, offset in enumerate(offs):
                    copy = pltpu.make_async_remote_copy(
                        src_ref=o_ref.at[pl.ds(at, length), :], dst_ref=o_ref.at[pl.ds(at, length), :],
                        send_sem=send.at[n], recv_sem=recv.at[n],
                        device_id=peer_of(stage, offset), device_id_type=MESH)
                    copy.start()
                    gath[c].append(copy)
                    pending.append(copy)
    for copy in pending:
        copy.wait_send()


def summed(x, colors, cid):
    scratch = []
    for start, rows, stages in colors:
        length = rows
        for stage in stages:
            length //= size_of(stage)
            n = size_of(stage) - 1
            assert length % 8 == 0
            scratch += [pltpu.VMEM((n, length, 128), jnp.float32), pltpu.VMEM((length, 128), jnp.float32)]
            scratch += [pltpu.SemaphoreType.DMA((n,))] * 4
    return pl.pallas_call(
        functools.partial(sum_kernel, colors),
        out_shape=jax.ShapeDtypeStruct(x.shape, x.dtype),
        in_specs=[pl.BlockSpec(memory_space=pltpu.VMEM)],
        out_specs=pl.BlockSpec(memory_space=pltpu.VMEM),
        scratch_shapes=scratch,
        compiler_params=pltpu.CompilerParams(collective_id=cid, has_side_effects=True, vmem_limit_bytes=50 * 2**20),
        name="summed%d" % cid,
    )(x)


G, X, Y, Z = "grp", "rows_2", "rows_1", "rows_0"
THREE = [((G,), (X,), (Y,), (Z,)), ((G,), (Y,), (Z,), (X,)), ((G,), (Z,), (X,), (Y,))]
ONE = [((G,), (X, Y, Z))]


def colored(rows, orders):
    each = rows // len(orders)
    return [(n * each, each, order) for n, order in enumerate(orders)]


def factor(work, upper_ref, inverse_ref):
    lane = lax.broadcasted_iota(jnp.int32, (BLOCK, PANEL), 1)
    sub = lax.broadcasted_iota(jnp.int32, (BLOCK, HALF), 0)
    lane_half = lax.broadcasted_iota(jnp.int32, (BLOCK, HALF), 1)
    for k in range(PANEL // BLOCK):
        at = k * BLOCK
        rows = work[at : at + BLOCK, :]
        base = at // HALF * HALF
        off = at - base
        diag = rows[:, base : base + HALF]
        cols = [jnp.broadcast_to(diag[:, off + j : off + j + 1], (BLOCK, HALF)) for j in range(BLOCK)]
        eye = (lane_half == sub + off).astype(jnp.float32)
        wide = [rows[:, :HALF], rows[:, HALF:]]
        own = base // HALF
        inside = (lane_half >= off) & (lane_half < off + BLOCK)
        wide[own] = jnp.where(inside, eye, wide[own])
        scale = jnp.zeros((BLOCK, HALF), jnp.float32)
        for j in range(BLOCK):
            pivot = jnp.broadcast_to(cols[j][j : j + 1, :], (BLOCK, HALF))
            scale = jnp.where(sub == j, pivot, scale)
            if j == BLOCK - 1:
                break
            ratio = cols[j] * (1.0 / pivot)
            ratio = jnp.where(sub > j, ratio, 0.0)
            for m in range(j + 1, BLOCK):
                cols[m] = cols[m] - ratio * jnp.broadcast_to(cols[j][m : m + 1, :], (BLOCK, HALF))
            for h in range(2):
                wide[h] = wide[h] - ratio * jnp.broadcast_to(wide[h][j : j + 1, :], (BLOCK, HALF))
            diag = diag - ratio * jnp.broadcast_to(diag[j : j + 1, :], (BLOCK, HALF))
        scale = lax.rsqrt(scale)
        done = jnp.concatenate([wide[0] * scale, wide[1] * scale], axis=1)
        inverse_ref[at : at + BLOCK, :] = jnp.where(lane < at + BLOCK, done, 0.0)
        upper_ref[at : at + BLOCK, :] = jnp.where(lane >= at + BLOCK, done, 0.0)
        upper_ref[at : at + BLOCK, base : base + HALF] = jnp.where(
            inside & (lane_half - off >= sub), diag * scale, upper_ref[at : at + BLOCK, base : base + HALF]
        )
        if at + BLOCK < PANEL:
            a, b, c = thirds(done)
            right = jnp.concatenate([a, b, a, c, a, b], axis=0)
            left = jnp.concatenate([a, a, b, a, c, b], axis=0)
            prod = lax.dot_general(left.T[at + BLOCK :, :], right, (((1,), (0,)), ((), ())), preferred_element_type=jnp.float32)
            rest = work[at + BLOCK :, :]
            lanes = lax.broadcasted_iota(jnp.int32, rest.shape, 1)
            rest = jnp.where((lanes >= at) & (lanes < at + BLOCK), 0.0, rest)
            work[at + BLOCK :, :] = rest - prod


WIDTH = 1024
STEP = 512
F32 = jnp.float32
BF16 = jnp.bfloat16
EARLY_ROWS = 9216
FIRST_ROWS = 1024
LAST_ROWS = 3072


def dot(left, right):
    return jnp.dot(left, right, preferred_element_type=F32)


def exact(left, right):
    return jnp.dot(left, right, precision=lax.Precision.HIGHEST, preferred_element_type=F32)


def pairs():
    return [(i, j) for i in range(4) for j in range(i, 4)]


def add_slabs(ref, at, value):
    rows = value.shape[0]
    for n in range(value.shape[1] // HALF):
        ref[at + n * rows : at + (n + 1) * rows, :] += value[:, n * HALF : (n + 1) * HALF]


def read_slabs(ref, at, rows, columns):
    return jnp.concatenate([ref[at + n * rows : at + (n + 1) * rows, :] for n in range(columns // HALF)], axis=1)


def products_kernel(earlier_ref, panels_ref, out_ref):
    @pl.when(pl.program_id(0) == 0)
    def _():
        out_ref[...] = jnp.zeros_like(out_ref)

    order = pairs()
    for i in range(4):
        turned = earlier_ref[:, i * PANEL : (i + 1) * PANEL].T
        value = dot(turned, panels_ref[...])
        for n in range(4):
            at = n * WIDTH + i * PANEL
            out_ref[at : at + PANEL, :] += value[:, n * HALF : (n + 1) * HALF]
        for j in range(i, 4):
            add_slabs(out_ref, 4 * WIDTH + order.index((i, j)) * 512, dot(turned, earlier_ref[:, j * PANEL : (j + 1) * PANEL]))


def add_gram(top, low, others, out_ref, mixed, at):
    top_t, low_t = top.T, low.T
    add_slabs(out_ref, at, dot(top_t, top) + dot(low_t, low))
    mixed[...] += dot(top_t, low)
    add_slabs(out_ref, at + 512, dot(top_t, others) + dot(low_t, others))


def close_gram(out_ref, mixed, at):
    value = mixed[...]
    add_slabs(out_ref, at, value + value.T)


def first_kernel(
    total, sums_ref, earlier_ref, panels_ref,
    top_ref, low_ref, flat_ref, early_ref, second_ref, left_ref, meet_ref, out_ref,
    coeffs, near, off_top, off_low, mixed,
):
    step = pl.program_id(0)

    @pl.when(step == 0)
    def _():
        scale = 1.0 / total
        for n, (i, j) in enumerate(pairs()):
            block = read_slabs(sums_ref, 4 * WIDTH + n * 512, PANEL, PANEL) * scale
            if i == j:
                rows = lax.broadcasted_iota(jnp.int32, block.shape, 0)
                columns = lax.broadcasted_iota(jnp.int32, block.shape, 1)
                block = block - (rows == columns).astype(F32)
            for r, c, value in [(i, j, block)] + ([(j, i, block.T)] if i != j else []):
                top, low = halves(value)
                off_top[r * PANEL : (r + 1) * PANEL, c * PANEL : (c + 1) * PANEL] = top
                off_low[r * PANEL : (r + 1) * PANEL, c * PANEL : (c + 1) * PANEL] = low
        for n in range(4):
            coeffs[:, n * HALF : (n + 1) * HALF] = (sums_ref[n * WIDTH : (n + 1) * WIDTH, :] * scale).astype(BF16)
        early = coeffs[...]
        for i in range(4):
            at = slice(i * PANEL, (i + 1) * PANEL)
            own = jnp.concatenate([sums_ref[n * WIDTH + i * PANEL : n * WIDTH + (i + 1) * PANEL, :] for n in range(4)], axis=1) * scale
            value = own - early[at, :].astype(F32) - (dot(off_top[at, :], early) + dot(off_low[at, :], early))
            near[at, :] = value[:, :PANEL].astype(BF16)
            left_ref[at, :] = value[:, :PANEL] - value[:, :PANEL].astype(BF16).astype(F32)
            second_ref[at, :] = value[:, PANEL:]
        meet = jnp.zeros((PANEL, PANEL), F32)
        for i in range(4):
            at = slice(i * PANEL, (i + 1) * PANEL)
            value = left_ref[at, :] - (dot(off_top[at, :], near[...]) + dot(off_low[at, :], near[...]))
            left_ref[at, :] = value
            top, low = halves(value.T)
            meet = meet + dot(top, early[at, PANEL:]) + dot(low, early[at, PANEL:])
        meet_ref[...] = meet
        early_ref[...] = early[:, PANEL:]
        out_ref[...] = jnp.zeros_like(out_ref)
        mixed[...] = jnp.zeros_like(mixed)

    space = earlier_ref[...]
    flat = panels_ref[...].astype(F32) - dot(space, coeffs[...])
    flat_ref[...] = flat[:, PANEL:]
    once = flat[:, :PANEL].astype(BF16)
    twice = once.astype(F32) - dot(space, near[...])
    top, low = halves(twice)
    top_ref[...] = top
    low_ref[...] = low
    add_gram(top, low, panels_ref[:, PANEL:], out_ref, mixed, 0)

    @pl.when(step == pl.num_programs(0) - 1)
    def _():
        close_gram(out_ref, mixed, 0)


def normalized(top, low, turned_top, turned_low):
    return (dot(top, turned_top) + (dot(top, turned_low) + dot(low, turned_top))).astype(BF16)


def second_kernel(
    total, sums_ref, left_ref, second_ref, meet_ref, earlier_ref, top_ref, low_ref, flat_ref, later_ref,
    upper_ref, basis_ref, newtop_ref, newlow_ref, out_ref,
    work, inverse, turned_top, turned_low, fresh_b, near_e, near_q, mixed,
):
    step = pl.program_id(0)

    @pl.when(step == 0)
    def _():
        scale = 1.0 / total
        work[...] = read_slabs(sums_ref, 0, PANEL, PANEL) * scale
        factor(work, upper_ref, inverse)
        turn = inverse[...].T
        turned_top[...], turned_low[...] = halves(turn)
        fresh = exact(inverse[...], read_slabs(sums_ref, 512, PANEL, PANEL) * scale)
        fresh_b[...] = fresh.astype(BF16)
        rounded = fresh.astype(BF16).astype(F32)
        near_q[...] = (fresh - rounded - exact(inverse[...], meet_ref[...])).astype(BF16)
        back = exact(turn, rounded)
        near_e[...] = (second_ref[...] - exact(left_ref[...], back)).astype(BF16)
        out_ref[...] = jnp.zeros_like(out_ref)
        mixed[...] = jnp.zeros_like(mixed)

    newcols = normalized(top_ref[...], low_ref[...], turned_top[...], turned_low[...])
    basis_ref[...] = newcols
    once = (flat_ref[...] - dot(newcols, fresh_b[...])).astype(BF16)
    twice = once.astype(F32) - (dot(earlier_ref[...], near_e[...]) + dot(newcols, near_q[...]))
    top, low = halves(twice)
    newtop_ref[...] = top
    newlow_ref[...] = low
    add_gram(top, low, later_ref[...], out_ref, mixed, 0)
    add_slabs(out_ref, 1536, dot(newcols.T, later_ref[...]))

    @pl.when(step == pl.num_programs(0) - 1)
    def _():
        close_gram(out_ref, mixed, 0)


def third_kernel(
    total, sums_ref, first_upper_ref, top_ref, low_ref, _, factors_ref, shift_ref, basis_ref,
    work, inverse, turned_top, turned_low,
):
    @pl.when(pl.program_id(0) == 0)
    def _():
        scale = 1.0 / total
        work[...] = read_slabs(sums_ref, 0, PANEL, PANEL) * scale
        factors_ref[0] = first_upper_ref[...]
        factor(work, factors_ref.at[1], inverse)
        turned_top[...], turned_low[...] = halves(inverse[...].T)
        shift_ref[:PANEL, :] = read_slabs(sums_ref, 1536, PANEL, 512) * scale
        shift_ref[PANEL:, :] = exact(inverse[...], read_slabs(sums_ref, 512, PANEL, 512) * scale)

    basis_ref[...] = normalized(top_ref[...], low_ref[...], turned_top[...], turned_low[...])


def whole(*shape):
    return pl.BlockSpec(shape, lambda n: (0,) * len(shape))


def rows(columns, place=0, step=STEP):
    return pl.BlockSpec((step, columns), lambda n: (n, place))


def shape(*lengths, dtype=F32):
    return jax.ShapeDtypeStruct(lengths, dtype)


def call(kernel, steps, name, **options):
    return pl.pallas_call(
        kernel,
        grid=(steps,),
        compiler_params=pltpu.CompilerParams(dimension_semantics=("arbitrary",), vmem_limit_bytes=56 * 2**20),
        name=name,
        **options,
    )


def body(earlier, snapshots, later):
    local = earlier.shape[0]
    total = local * lax.axis_size(AXES)
    steps = local // STEP
    square = pltpu.VMEM((PANEL, PANEL), F32)
    small = pltpu.VMEM((PANEL, PANEL), BF16)

    partial = call(
        products_kernel, local // 1024, "products",
        in_specs=[rows(WIDTH, step=1024), rows(512, step=1024)],
        out_specs=whole(EARLY_ROWS, HALF),
        out_shape=shape(EARLY_ROWS, HALF),
    )(earlier, snapshots)
    early_sums = summed(partial, colored(EARLY_ROWS, THREE), 1)
    top, low, flat, early, second, left, meet, partial = call(
        functools.partial(first_kernel, total), steps, "first",
        in_specs=[whole(EARLY_ROWS, HALF), rows(WIDTH), rows(512)],
        out_specs=[rows(PANEL), rows(PANEL), rows(PANEL), whole(WIDTH, PANEL), whole(WIDTH, PANEL), whole(WIDTH, PANEL),
                   whole(PANEL, PANEL), whole(FIRST_ROWS, HALF)],
        out_shape=[shape(local, PANEL, dtype=BF16), shape(local, PANEL, dtype=BF16), shape(local, PANEL),
                   shape(WIDTH, PANEL, dtype=BF16), shape(WIDTH, PANEL), shape(WIDTH, PANEL), shape(PANEL, PANEL),
                   shape(FIRST_ROWS, HALF)],
        scratch_shapes=[pltpu.VMEM((WIDTH, 512), BF16), pltpu.VMEM((WIDTH, PANEL), BF16), pltpu.VMEM((WIDTH, WIDTH), BF16),
                        pltpu.VMEM((WIDTH, WIDTH), BF16), square],
    )(early_sums, earlier, snapshots)
    first_sums = summed(partial, colored(FIRST_ROWS, ONE), 2)
    upper, basis, newtop, newlow, partial = call(
        functools.partial(second_kernel, total), steps, "second",
        in_specs=[whole(FIRST_ROWS, HALF), whole(WIDTH, PANEL), whole(WIDTH, PANEL), whole(PANEL, PANEL), rows(WIDTH),
                  rows(PANEL), rows(PANEL), rows(PANEL), rows(512)],
        out_specs=[whole(PANEL, PANEL), rows(PANEL), rows(PANEL), rows(PANEL), whole(LAST_ROWS, HALF)],
        out_shape=[shape(PANEL, PANEL), shape(local, 512, dtype=BF16), shape(local, PANEL, dtype=BF16),
                   shape(local, PANEL, dtype=BF16), shape(LAST_ROWS, HALF)],
        scratch_shapes=[square, square, small, small, small, pltpu.VMEM((WIDTH, PANEL), BF16), small, square],
    )(first_sums, left, second, meet, earlier, top, low, flat, later)
    last_sums = summed(partial, colored(LAST_ROWS, ONE), 3)
    factors, shift_block, basis = call(
        functools.partial(third_kernel, total), steps, "third",
        in_specs=[whole(LAST_ROWS, HALF), whole(PANEL, PANEL), rows(PANEL), rows(PANEL), pl.BlockSpec(memory_space=pl.ANY)],
        out_specs=[whole(2, PANEL, PANEL), whole(512, 512), rows(PANEL, 1)],
        out_shape=[shape(2, PANEL, PANEL), shape(512, 512), shape(local, 512, dtype=BF16)],
        scratch_shapes=[square, square, small, small],
        input_output_aliases={4: 2},
    )(last_sums, upper, newtop, newlow, basis)
    return (basis, factors, shift_block)


def solution(mesh):
    torus = Mesh(mesh.devices.reshape(4, 4, 4, mesh.shape["grp"]), AXES)
    spec = P(AXES, None)
    return jax.shard_map(
        body, mesh=torus, in_specs=(spec, spec, spec), out_specs=(spec, P(), P()), check_vma=False
    )
```

time: 568 us -> 216 us (0.38); the launches traced: 558 us -> 216 us
  blocking collectives: 234 us -> 0 us
  Pallas kernels: 0 us -> 210 us
  other arithmetic: 121 us -> 0 us
  matrix products: 78.7 us -> 0 us
  local copies, waits for them, and re-layouts: 48.8 us -> 4.39 us
  waiting for transfers between devices: 42 us -> 0 us
  starting transfers between devices: 28.9 us -> 0 us
    all_to_all x22 -> x0, blocking collectives: 234 us -> none  [the longest x6 108 us: summed_rows(): lax.all_to_all(nearer, far, split_axis=0, concat_axis=0, tiled=True)]
    pallas_call x0 -> x7, Pallas kernels: none -> 210 us  [the longest x3 121 us: summed(): pl.pallas_call(functools.partial(sum_kernel, colors), out_shape=jax.Shape...]
    another operation x20 -> x0, other arithmetic: 111 us -> none  [the longest x13 68.5 us: factor(): lower = jnp.linalg.cholesky(gram)]
    dot_general x13 -> x0, matrix products: 76 us -> none  [the longest x4 25 us: applied(): jnp.dot(space, coeffs.astype(jnp.bfloat16), preferred_element_type=jnp.fl...]
    all_to_all x6 -> x0, waiting for transfers between devices: 42 us -> none  [the longest x4 29 us: copy_for_each(): return lax.all_to_all(copies, axis, split_axis=0, concat_axis=0, tiled=True)]
    all_to_all x6 -> x0, starting transfers between devices: 28.9 us -> none  [the longest x4 19.1 us: copy_for_each(): return lax.all_to_all(copies, axis, split_axis=0, concat_axis=0, tiled=True)]
    another operation x29 -> x0, local copies, waits for them, and re-layouts: 14.4 us -> none  [the longest x15 8.2 us: factor(): jax.scipy.linalg.solve_triangular(lower, jnp.eye(gram.shape[0], dtype=jnp...]
    unnamed x35 -> x8, local copies, waits for them, and re-layouts: 18.3 us -> 4.39 us
  transfers between devices with their start and end apart: 6 -> 0, of which waited for: 6 -> 0; matrix products, arithmetic and copies ran while one was open for 3% -> 0% of each run, Pallas kernels for 0% -> 0%
where the time goes in v1:
time: 216 us
  Pallas kernels  210 us (97%)
  local copies, waits for them, and re-layouts  4.39 us (2%)
    pallas_call x3, Pallas kernels, summed(): pl.pallas_call(functools.partial(sum_kernel, colors), out_shape=jax.Shape...  121 us
    pallas_call x1, Pallas kernels, body(): call(functools.partial(second_kernel, total), steps, 'second', in_specs=[...  32 us
    pallas_call x1, Pallas kernels, body(): call(functools.partial(first_kernel, total), steps, 'first', in_specs=[wh...  27.6 us
    pallas_call x1, Pallas kernels, body(): call(products_kernel, local // 1024, 'products', in_specs=[rows(WIDTH, st...  15 us
    pallas_call x1, Pallas kernels, body(): call(functools.partial(third_kernel, total), steps, 'third', in_specs=[wh...  15 us
    unnamed x8, local copies, waits for them, and re-layouts  4.39 us

profile of v1, /device:TPU:1, one launch (start us, length us, event | category | flops | bytes accessed | tf_op | source)
XLA Modules:
  0.0 215.6 jit_solution(13249020424904509658)
XLA Ops:
  0.6 15.0 %products.1.x_ref = f32[9216,128]{1,0:T(8,128)} custom-call(bf16[4096,1024]{1,0:T(8,128)(2,1)} %earlier_ref.5, bf16[4096,512]{1,0:T(8,128)(2,1)} %panels_ref.3), custom_call_target="tpu_custom_call" | custom-call | tf_op jit(solution)/shard_map/products/pallas_call | solution.py:434
  15.6 58.1 %summed1.1.sums_ref = f32[9216,128]{1,0:T(8,128)} custom-call(f32[9216,128]{1,0:T(8,128)} %products.1.x_ref), custom_call_target="tpu_custom_call" | custom-call | tf_op jit(solution)/shard_map/summed1/pallas_call | solution.py:162
  73.7 27.6 %first.1 = (bf16[4096,256]{1,0:T(8,128)(2,1)}, bf16[4096,256]{1,0:T(8,128)(2,1)}, f32[4096,256]{1,0:T(8,128)}, bf16[1024,256]{1,0:T(8,128)(2,1)}, f32[1024,256]{...) custom-call(f32[9216,128]{1,0:T(8,128)} %summed1.1.sums_ref, ...), custom_call_target="tpu_custom_call" | custom-call | tf_op jit(solution)/shard_map/first/pallas_call | solution.py:441
  101.3 0.0 copy-start.3
  101.3 1.0 copy-done.3
  102.3 25.2 %summed2.1.sums_ref = f32[1024,128]{1,0:T(8,128)S(1)} custom-call(f32[1024,128]{1,0:T(8,128)S(1)} %copy-done.3), custom_call_target="tpu_custom_call" | custom-call | tf_op jit(solution)/shard_map/summed2/pallas_call | solution.py:162
  127.5 0.0 copy-start.1
  127.5 0.8 copy-done.1
  128.3 32.0 %second.1 = (f32[256,256]{1,0:T(8,128)}, bf16[4096,512]{1,0:T(8,128)(2,1)}, bf16[4096,256]{1,0:T(8,128)(2,1)}, bf16[4096,256]{1,0:T(8,128)(2,1)}, f32[3072,128]{1,0:T(8,128)}) custom-call(f32[1024,128]{1,0:T(8,128)} %copy-done.1, f32[1024,256]{1,0:T(8,128)} %get-tuple-element.19.left_ref, f32[1024,256]{1,0:T(8,128)} %get-tuple-element.20.second_ref, ...), custom_call_target="tpu_custom_call" | custom-call | tf_op jit(solution)/shard_map/second/pallas_call | solution.py:453
  160.4 0.0 copy-start.2
  160.4 1.4 copy-done.2
  161.8 37.6 %summed3.1.sums_ref = f32[3072,128]{1,0:T(8,128)S(1)} custom-call(f32[3072,128]{1,0:T(8,128)S(1)} %copy-done.2), custom_call_target="tpu_custom_call" | custom-call | tf_op jit(solution)/shard_map/summed3/pallas_call | solution.py:162
  199.4 0.0 copy-start
  199.4 1.2 copy-done
  200.6 15.0 %third.1 = (f32[2,256,256]{2,1,0:T(8,128)}, f32[512,512]{1,0:T(8,128)}, bf16[4096,512]{1,0:T(8,128)(2,1)}) custom-call(f32[3072,128]{1,0:T(8,128)} %copy-done, f32[256,256]{1,0:T(8,128)} %get-tuple-element.26.first_upper_ref, bf16[4096,256]{1,0:T(8,128)(2,1)} %get-tuple-element.27.top_ref, ...), custom_call_target="tpu_custom_call", output_to_operand_aliasing={{2}: (4, {})} | custom-call | tf_op jit(solution)/shard_map/third/pallas_call | solution.py:463
Async XLA Ops:
  101.3 1.0 copy-start.3
  127.5 0.8 copy-start.1
  160.4 1.4 copy-start.2
  199.4 1.2 copy-start
